TPU v7x, 32 devices: a whole 2x2x4 slice. The times are simulated.
32 devices in a mesh: row: 8 (over z, core), col: 4 (over y, x).
Axes of the slice: x: 2, y: 2, z: 4, core: 2. Of those that a mesh axis runs over, the one named last changes fastest.
Arguments:
- object_field: float32 [3, 2, 1024, 512], P(None, None, 'row', 'col'), may hold values from -5 to 5
- probe: float32 [2, 128, 128], replicated, may hold values from -5 to 5
- measured: float32 [8, 4, 2, 128, 128], P('row', 'col'), may hold values from 0.25 to 4
- positions: int32 [8, 4, 2, 2], P('row', 'col'), may hold values from 0 to 127
- counts: int32 [8, 4], P('row', 'col'), may hold values from 1 to 2, as said below
Outputs:
- object_next: float32 [3, 2, 1024, 512], P(None, None, 'row', 'col')
Inputs may be any that keep to these rules, and one draw needn't show every extreme that they name: Slots 0 to counts - 1 of a tile are live; some tile has all 2 live.
All inputs are finite; a program needn't handle non-finite values.
Results may differ from a plain program's by a relative error of at most 0.0003.
Values sent between devices are 32-bit elements; how exact they have to be, the bound alone decides.
A program may use at most 64 MiB of HBM per device.

v0:
```python
import math

import jax
import jax.numpy as jnp
from jax import lax
from jax.sharding import PartitionSpec as P

ITERS = 2


LEARNING_RATE = 0.02
PRECISE = lax.Precision.HIGHEST


def passed_along(block, axis, distance):
    devices = range(lax.axis_size(axis))
    route = [(i - distance, i) for i in devices if i - distance in devices]
    return lax.ppermute(block, axis, route)


def padded(block, sides, width):
    for axis, dim in sides:
        count = lax.axis_size(axis)
        forward = [(i, i + 1) for i in range(count - 1)]
        backward = [(target, source) for source, target in forward]
        low = lax.ppermute(
            lax.slice_in_dim(block, block.shape[dim] - width, None, axis=dim), axis, forward
        )
        high = lax.ppermute(lax.slice_in_dim(block, 0, width, axis=dim), axis, backward)
        block = jnp.concatenate([low, block, high], axis=dim)
    return block


def make_tables(window_side):
    ordinal = jnp.arange(window_side, dtype=jnp.int32)
    product = ordinal[:, None] * ordinal[None, :] % window_side
    angles = -2.0 * math.pi / window_side * product.astype(jnp.float32)
    norming = 1.0 / math.sqrt(window_side)
    frequency = (ordinal + window_side // 2) % window_side - window_side // 2
    squares = (
        frequency[:, None] * frequency[:, None] + frequency[None, :] * frequency[None, :]
    ).astype(jnp.float32)
    phases = -0.25 * math.pi / window_side * squares
    return (jnp.cos(angles) * norming, jnp.sin(angles) * norming, jnp.cos(phases), jnp.sin(phases))


def right_mul(values, matrix):
    return jnp.einsum("...n,nk->...k", values, matrix, precision=PRECISE)


def left_mul(values, matrix):
    return jnp.einsum("...nm,nk->...km", values, matrix, precision=PRECISE)


def complex_times(left_pair, right_pair):
    return (
        left_pair[0] * right_pair[0] - left_pair[1] * right_pair[1],
        left_pair[0] * right_pair[1] + left_pair[1] * right_pair[0],
    )


def conj_times(left_pair, right_pair):
    return (
        left_pair[0] * right_pair[0] + left_pair[1] * right_pair[1],
        left_pair[0] * right_pair[1] - left_pair[1] * right_pair[0],
    )


def transform(pair, tables, sign):
    real_part, imag_part = pair
    for multiply in (right_mul, left_mul):
        real_cos = multiply(real_part, tables[0])
        real_sin = multiply(real_part, tables[1])
        imag_cos = multiply(imag_part, tables[0])
        imag_sin = multiply(imag_part, tables[1])
        real_part, imag_part = (real_cos - sign * imag_sin, imag_cos + sign * real_sin)
    return (real_part, imag_part)


def propagate(pair, tables, sign):
    spectrum = transform(pair, tables, 1.0)
    kernel = (tables[2], sign * tables[3])
    return transform(complex_times(kernel, spectrum), tables, -1.0)


def slot_gradients(windows, probe, samples, tables):
    layer_count = windows.shape[1]
    layers = [
        (windows[:, slice_index, 0], windows[:, slice_index, 1])
        for slice_index in range(layer_count)
    ]
    wavefield = (
        jnp.broadcast_to(probe[0], samples.shape),
        jnp.broadcast_to(probe[1], samples.shape),
    )
    incident = []
    for slice_index in range(layer_count):
        incident.append(wavefield)
        wavefield = complex_times(layers[slice_index], wavefield)
        if slice_index + 1 < layer_count:
            wavefield = propagate(wavefield, tables, 1.0)
    far_field = transform(wavefield, tables, 1.0)
    residue = far_field[0] * far_field[0] + far_field[1] * far_field[1] - samples
    back_wave = transform((residue * far_field[0], residue * far_field[1]), tables, -1.0)
    pieces = [None] * layer_count
    for slice_index in reversed(range(layer_count)):
        product = conj_times(incident[slice_index], back_wave)
        pieces[slice_index] = jnp.stack(product, axis=1)
        if slice_index > 0:
            back_wave = propagate(conj_times(layers[slice_index], back_wave), tables, -1.0)
    return jnp.stack(pieces, axis=1)


def add_window(running, update, corner):
    anchor = jnp.zeros((), jnp.int32)
    corner_start = (anchor, anchor, corner[0], corner[1])
    before = lax.dynamic_slice(running, corner_start, update.shape)
    return lax.dynamic_update_slice(running, before + update, corner_start)


def fold_rows(gradient_sum, rim_width):
    inner_size = gradient_sum.shape[2] - 2 * rim_width
    from_below = passed_along(gradient_sum[:, :, :rim_width], "row", -1)
    from_above = passed_along(gradient_sum[:, :, rim_width + inner_size :], "row", 1)
    interior = gradient_sum[:, :, rim_width : rim_width + inner_size]
    interior = interior.at[:, :, inner_size - rim_width :].add(from_below)
    interior = interior.at[:, :, :rim_width].add(from_above)
    return interior


def fold_cols(gradient_sum, rim_width):
    inner_size = gradient_sum.shape[3] - 2 * rim_width
    from_right = passed_along(gradient_sum[:, :, :, :rim_width], "col", -1)
    from_left = passed_along(gradient_sum[:, :, :, rim_width + inner_size :], "col", 1)
    interior = gradient_sum[:, :, :, rim_width : rim_width + inner_size]
    interior = interior.at[:, :, :, inner_size - rim_width :].add(from_right)
    interior = interior.at[:, :, :, :rim_width].add(from_left)
    return interior


def shards(object_field, probe, measured, positions, counts):
    layer_count = object_field.shape[0]
    window_side = probe.shape[-1]
    rim_width = window_side // 2
    tables = make_tables(window_side)
    corners = positions[0, 0]
    samples = measured[0, 0]
    live_count = counts[0, 0]
    slot_count = corners.shape[0]
    window_shape = (layer_count, 2, window_side, window_side)
    anchor = jnp.zeros((), jnp.int32)
    current = object_field
    for iteration in range(ITERS):
        extended = padded(current, (("row", 2), ("col", 3)), rim_width)
        gradient_sum = jnp.zeros_like(extended)
        windows = jax.vmap(
            lambda corner: lax.dynamic_slice(
                extended, (anchor, anchor, corner[0], corner[1]), window_shape
            )
        )(corners)
        live_mask = (jnp.arange(slot_count, dtype=jnp.int32) < live_count).astype(jnp.float32)
        gradients = (
            slot_gradients(windows, probe, samples, tables) * live_mask[:, None, None, None, None]
        )
        for slot_index in range(slot_count):
            gradient_sum = add_window(gradient_sum, gradients[slot_index], corners[slot_index])
        summed = fold_cols(fold_rows(gradient_sum, rim_width), rim_width)
        current = current - LEARNING_RATE * summed
    return current


def solution(mesh):
    placed = (
        P(None, None, "row", "col"),
        P(),
        P("row", "col", None, None, None),
        P("row", "col", None, None),
        P("row", "col"),
    )
    return jax.shard_map(
        shards, mesh=mesh, in_specs=placed, out_specs=P(None, None, "row", "col"), check_vma=False
    )
```

profile of v0, /device:TPU:18, one launch (start us, length us, event | category | flops | bytes accessed | tf_op | source)
XLA Modules:
  0.0 288.7 jit_solution(3623526778286126693)
XLA Ops:
  3.3 3.6 %collective-permute-start.1 = (f32[3,2,64,128]{2,3,1,0:T(8,128)S(1)}, f32[3,2,64,128]{2,3,1,0:T(8,128)S(1)}, u32[]{:S(2)}, u32[]{:S(2)}) collective-permute-start(f32[3,2,64,128]{2,3,1,0:T(8,128)S(1)} %get-tuple-element.184), channel_id=1, source_target_pairs={{4,0},{8,4},{12,8},{16,12},{20,16},{24,20},{28,24},{5,1},{9,5},{13... | collective-permute-start | bytes 589832 | tf_op jit(solution)/shard_map/ppermute | solution.py:29
  27.2 8.0 %collective-permute-done.3 = f32[3,2,256,64]{2,3,1,0:T(8,128)} collective-permute-done((f32[3,2,256,64]{2,3,1,0:T(8,128)S(1)}, f32[3,2,256,64]{2,3,1,0:T(8,128)}, u32[]{:S(2)}, u32[]{:S(2)}) %collective-permute-start.3) | collective-permute-done | bytes 393248 | tf_op jit(solution)/shard_map/ppermute | solution.py:29
  36.6 6.8 %while.10 = (s32[]{:T(128)}, f32[3,2,256,256]{2,3,1,0:T(8,128)S(1)}, s32[2,4]{1,0:T(2,128)S(1)}, f32[2,3,2,128,128]{4,3,0,2,1:T(8,128)}, s32[]{:T(128)}) while((s32[]{:T(128)}, f32[3,2,256,256]{2,3,1,0:T(8,128)S(1)}, s32[2,4]{1,0:T(2,128)S(1)}, f32[2,3,2,128,128]{4,3,0,2,1:T(8,128)}, s32[]{:T(128)}) %tuple.108), condition=%wide.while_cond.8, body=%wide.while_body.8.sunk | while | flops 2 | bytes 8650933 | solution.py:157
  89.4 9.9 %dynamic_update_slice.12 = f32[3,2,256,256]{3,2,1,0:T(8,128)S(1)} dynamic-update-slice(f32[3,2,256,256]{3,2,1,0:T(8,128)S(1)} %broadcast.353.clone, f32[3,2,128,128]{3,2,1,0:T(8,128)S(1)} %slice_bitcast_fusion.3, s32[]{:T(128)} %constant.221.clone.1, s32[]{:T(128)} %constant.221.clone.1, s32[]{:T(128)S(6)} %select_n.435, s32[]{:T(128)S(6)} %select_n.436) | dynamic-update-slice | bytes 786436 | tf_op jit(solution)/shard_map/dynamic_update_slice | solution.py:118
  99.6 9.9 %dynamic_update_slice.13 = f32[3,2,256,256]{3,2,1,0:T(8,128)S(1)} dynamic-update-slice(f32[3,2,256,256]{3,2,1,0:T(8,128)S(1)} %dynamic_update_slice.12, f32[3,2,128,128]{3,2,1,0:T(8,128)S(1)} %fusion.25, s32[]{:T(128)} %constant.221.clone.1, s32[]{:T(128)} %constant.221.clone.1, s32[]{:T(128)S(6)} %select_n.437, s32[]{:T(128)S(6)} %select_n.438) | dynamic-update-slice | bytes 786436 | tf_op jit(solution)/shard_map/dynamic_update_slice | solution.py:118
  109.6 5.5 %collective-permute-start.4 = (f32[3,2,64,256]{3,2,1,0:T(8,128)S(1)}, f32[3,2,64,256]{3,2,1,0:T(8,128)S(1)}, u32[]{:S(2)}, u32[]{:S(2)}) collective-permute-start(f32[3,2,64,256]{3,2,1,0:T(8,128)S(1)} %get-tuple-element.144), channel_id=1, source_target_pairs={{4,0},{8,4},{12,8},{16,12},{20,16},{24,20},{28,24},{5,1},{9,5},{13... | collective-permute-start | bytes 1179656 | tf_op jit(solution)/shard_map/ppermute | solution.py:18
  120.4 3.8 %collective-permute-done.5 = f32[3,2,64,256]{3,2,1,0:T(8,128)S(1)} collective-permute-done((f32[3,2,64,256]{3,2,1,0:T(8,128)S(1)}, f32[3,2,64,256]{3,2,1,0:T(8,128)S(1)}, u32[]{:S(2)}, u32[]{:S(2)}) %collective-permute-start.5) | collective-permute-done | bytes 393248 | tf_op jit(solution)/shard_map/ppermute | solution.py:18
  127.1 4.2 %collective-permute-start.7 = (f32[3,2,128,64]{3,2,1,0:T(8,128)S(1)}, f32[3,2,128,64]{3,2,1,0:T(8,128)S(1)}, u32[]{:S(2)}, u32[]{:S(2)}) collective-permute-start(f32[3,2,128,64]{3,2,1,0:T(8,128)S(1)} %get-tuple-element.165), channel_id=1, source_target_pairs={{0,1},{1,2},{2,3},{4,5},{5,6},{6,7},{8,9},{9,10},{10,11},{12,13},{... | collective-permute-start | bytes 589832 | tf_op jit(solution)/shard_map/ppermute | solution.py:18
  131.3 7.9 %collective-permute-done.6 = f32[3,2,128,64]{3,2,1,0:T(8,128)S(1)} collective-permute-done((f32[3,2,128,64]{3,2,1,0:T(8,128)S(1)}, f32[3,2,128,64]{3,2,1,0:T(8,128)S(1)}, u32[]{:S(2)}, u32[]{:S(2)}) %collective-permute-start.6) | collective-permute-done | bytes 196640 | tf_op jit(solution)/shard_map/ppermute | solution.py:18
  139.3 4.6 %scatter-add.30 = f32[3,2,128,128]{3,2,1,0:T(8,128)S(1)} dynamic-update-slice(f32[3,2,128,128]{3,2,1,0:T(8,128)S(1)} %slice.491, f32[3,2,128,64]{3,2,1,0:T(8,128)S(1)} %slice_add_fusion.5, s32[]{:T(128)} %constant.221.clone.1, s32[]{:T(128)} %constant.221.clone.1, s32[]{:T(128)} %constant.221.clone.1, s32[]{:T(128)} %constant.226.clone.1) | dynamic-update-slice | bytes 393220 | tf_op jit(solution)/shard_map/scatter-add | solution.py:136
  144.1 3.5 %scatter-add.31 = f32[3,2,128,128]{3,2,1,0:T(8,128)S(1)} dynamic-update-slice(f32[3,2,128,128]{3,2,1,0:T(8,128)S(1)} %scatter-add.30, f32[3,2,128,64]{3,2,1,0:T(8,128)S(1)} %slice_add_fusion.4, s32[]{:T(128)} %constant.221.clone.1, s32[]{:T(128)} %constant.221.clone.1, s32[]{:T(128)} %constant.221.clone.1, s32[]{:T(128)} %constant.221.clone.1) | dynamic-update-slice | bytes 393220 | tf_op jit(solution)/shard_map/scatter-add | solution.py:137
  149.6 3.6 %collective-permute-start.9 = (f32[3,2,64,128]{3,2,1,0:T(8,128)S(1)}, f32[3,2,64,128]{3,2,1,0:T(8,128)S(1)}, u32[]{:S(2)}, u32[]{:S(2)}) collective-permute-start(f32[3,2,64,128]{3,2,1,0:T(8,128)S(1)} %get-tuple-element.180), channel_id=1, source_target_pairs={{4,0},{8,4},{12,8},{16,12},{20,16},{24,20},{28,24},{5,1},{9,5},{13... | collective-permute-start | bytes 589832 | tf_op jit(solution)/shard_map/ppermute | solution.py:29
  157.7 5.3 %collective-permute-start.10 = (f32[3,2,256,64]{2,3,1,0:T(8,128)S(1)}, f32[3,2,256,64]{2,3,1,0:T(8,128)S(1)}, u32[]{:S(2)}, u32[]{:S(2)}) collective-permute-start(f32[3,2,256,64]{2,3,1,0:T(8,128)S(1)} %copy.154), channel_id=1, source_target_pairs={{0,1},{1,2},{2,3},{4,5},{5,6},{6,7},{8,9},{9,10},{10,11},{12,13},{... | collective-permute-start | bytes 1179656 | tf_op jit(solution)/shard_map/ppermute | solution.py:26
  165.2 7.3 %collective-permute-done.10 = f32[3,2,256,64]{2,3,1,0:T(8,128)S(1)} collective-permute-done((f32[3,2,256,64]{2,3,1,0:T(8,128)S(1)}, f32[3,2,256,64]{2,3,1,0:T(8,128)S(1)}, u32[]{:S(2)}, u32[]{:S(2)}) %collective-permute-start.10) | collective-permute-done | bytes 393248 | tf_op jit(solution)/shard_map/ppermute | solution.py:26
  173.6 6.5 %collective-permute-done.11 = f32[3,2,256,64]{2,3,1,0:T(8,128)S(1)} collective-permute-done((f32[3,2,256,64]{2,3,1,0:T(8,128)S(1)}, f32[3,2,256,64]{2,3,1,0:T(8,128)S(1)}, u32[]{:S(2)}, u32[]{:S(2)}) %collective-permute-start.11) | collective-permute-done | bytes 393248 | tf_op jit(solution)/shard_map/ppermute | solution.py:29
  183.4 4.4 %while.11 = (s32[]{:T(128)}, f32[3,2,256,256]{3,2,1,0:T(8,128)S(1)}, s32[2,4]{1,0:T(2,128)S(1)}, f32[2,3,2,128,128]{4,3,2,1,0:T(8,128)S(1)}, s32[]{:T(128)}) while((s32[]{:T(128)}, f32[3,2,256,256]{3,2,1,0:T(8,128)S(1)}, s32[2,4]{1,0:T(2,128)S(1)}, f32[2,3,2,128,128]{4,3,2,1,0:T(8,128)S(1)}, s32[]{:T(128)}) %tuple.114), condition=%wide.while_cond.9, body=%wide.while_body.9.sunk | while | flops 2 | bytes 786557 | solution.py:157
  231.6 8.8 %dynamic_update_slice.14 = f32[3,2,256,256]{3,2,1,0:T(8,128)S(1)} dynamic-update-slice(f32[3,2,256,256]{3,2,1,0:T(8,128)S(1)} %broadcast.353, f32[3,2,128,128]{3,2,1,0:T(8,128)} %slice_bitcast_fusion.1, s32[]{:T(128)} %constant.221.clone.1, s32[]{:T(128)} %constant.221.clone.1, s32[]{:T(128)S(6)} %select_n.435, s32[]{:T(128)S(6)} %select_n.436) | dynamic-update-slice | bytes 786436 | tf_op jit(solution)/shard_map/dynamic_update_slice | solution.py:118
  241.3 8.7 %dynamic_update_slice.15 = f32[3,2,256,256]{3,2,1,0:T(8,128)S(1)} dynamic-update-slice(f32[3,2,256,256]{3,2,1,0:T(8,128)S(1)} %dynamic_update_slice.14, f32[3,2,128,128]{3,2,1,0:T(8,128)} %fusion.22, s32[]{:T(128)} %constant.221.clone.1, s32[]{:T(128)} %constant.221.clone.1, s32[]{:T(128)S(6)} %select_n.437, s32[]{:T(128)S(6)} %select_n.438) | dynamic-update-slice | bytes 786436 | tf_op jit(solution)/shard_map/dynamic_update_slice | solution.py:118
  250.1 5.9 %collective-permute-start.12 = (f32[3,2,64,256]{3,2,1,0:T(8,128)S(1)}, f32[3,2,64,256]{3,2,1,0:T(8,128)S(1)}, u32[]{:S(2)}, u32[]{:S(2)}) collective-permute-start(f32[3,2,64,256]{3,2,1,0:T(8,128)S(1)} %get-tuple-element.142), channel_id=1, source_target_pairs={{4,0},{8,4},{12,8},{16,12},{20,16},{24,20},{28,24},{5,1},{9,5},{13... | collective-permute-start | bytes 1179656 | tf_op jit(solution)/shard_map/ppermute | solution.py:18
  261.4 3.8 %collective-permute-done.13 = f32[3,2,64,256]{3,2,1,0:T(8,128)S(1)} collective-permute-done((f32[3,2,64,256]{3,2,1,0:T(8,128)S(1)}, f32[3,2,64,256]{3,2,1,0:T(8,128)S(1)}, u32[]{:S(2)}, u32[]{:S(2)}) %collective-permute-start.13) | collective-permute-done | bytes 393248 | tf_op jit(solution)/shard_map/ppermute | solution.py:18
  267.5 4.8 %collective-permute-start.15 = (f32[3,2,128,64]{3,2,1,0:T(8,128)S(1)}, f32[3,2,128,64]{3,2,1,0:T(8,128)S(1)}, u32[]{:S(2)}, u32[]{:S(2)}) collective-permute-start(f32[3,2,128,64]{3,2,1,0:T(8,128)S(1)} %get-tuple-element.161), channel_id=1, source_target_pairs={{0,1},{1,2},{2,3},{4,5},{5,6},{6,7},{8,9},{9,10},{10,11},{12,13},{... | collective-permute-start | bytes 589832 | tf_op jit(solution)/shard_map/ppermute | solution.py:18
  272.3 7.1 %collective-permute-done.14 = f32[3,2,128,64]{3,2,1,0:T(8,128)S(1)} collective-permute-done((f32[3,2,128,64]{3,2,1,0:T(8,128)S(1)}, f32[3,2,128,64]{3,2,1,0:T(8,128)S(1)}, u32[]{:S(2)}, u32[]{:S(2)}) %collective-permute-start.14) | collective-permute-done | bytes 196640 | tf_op jit(solution)/shard_map/ppermute | solution.py:18
  279.5 4.6 %scatter-add.36 = f32[3,2,128,128]{3,2,1,0:T(8,128)S(1)} dynamic-update-slice(f32[3,2,128,128]{3,2,1,0:T(8,128)S(1)} %slice.512, f32[3,2,128,64]{3,2,1,0:T(8,128)S(1)} %slice_add_fusion.1, s32[]{:T(128)} %constant.221.clone.1, s32[]{:T(128)} %constant.221.clone.1, s32[]{:T(128)} %constant.221.clone.1, s32[]{:T(128)} %constant.226.clone.1) | dynamic-update-slice | bytes 393220 | tf_op jit(solution)/shard_map/scatter-add | solution.py:136
  284.2 3.5 %scatter-add.39 = f32[3,2,128,128]{3,2,1,0:T(8,128)S(1)} dynamic-update-slice(f32[3,2,128,128]{3,2,1,0:T(8,128)S(1)} %scatter-add.36, f32[3,2,128,64]{3,2,1,0:T(8,128)S(1)} %slice_add_fusion, s32[]{:T(128)} %constant.221.clone.1, s32[]{:T(128)} %constant.221.clone.1, s32[]{:T(128)} %constant.221.clone.1, s32[]{:T(128)} %constant.221.clone.1) | dynamic-update-slice | bytes 393220 | tf_op jit(solution)/shard_map/scatter-add | solution.py:137
  (268 shorter events, 147.0 us)
Async XLA Ops:
  0.0 7.0 %copy-start.7 = (s32[1,1,2,2]{3,2,1,0:T(2,128)S(1)}, s32[1,1,2,2]{3,2,1,0:T(2,128)}, u32[]{:S(2)}) copy-start(s32[1,1,2,2]{3,2,1,0:T(2,128)} %param.24) | copy-start | bytes 52
  0.0 7.7 %copy-start.6 = (f32[2,128,128]{2,1,0:T(8,128)S(1)}, f32[2,128,128]{2,1,0:T(8,128)}, u32[]{:S(2)}) copy-start(f32[2,128,128]{2,1,0:T(8,128)} %param.22) | copy-start | bytes 393220
  1.4 9.1 %collective-permute-start = (f32[3,2,64,128]{2,3,1,0:T(8,128)S(1)}, f32[3,2,64,128]{2,3,1,0:T(8,128)S(1)}, u32[]{:S(2)}, u32[]{:S(2)}) collective-permute-start(f32[3,2,64,128]{2,3,1,0:T(8,128)S(1)} %get-tuple-element.183), channel_id=1, source_target_pairs={{0,4},{4,8},{8,12},{12,16},{16,20},{20,24},{24,28},{1,5},{5,9},{9,... | collective-permute-start | bytes 589832 | tf_op jit(solution)/shard_map/ppermute | solution.py:26
  3.3 8.9 %collective-permute-start.1 = (f32[3,2,64,128]{2,3,1,0:T(8,128)S(1)}, f32[3,2,64,128]{2,3,1,0:T(8,128)S(1)}, u32[]{:S(2)}, u32[]{:S(2)}) collective-permute-start(f32[3,2,64,128]{2,3,1,0:T(8,128)S(1)} %get-tuple-element.184), channel_id=1, source_target_pairs={{4,0},{8,4},{12,8},{16,12},{20,16},{24,20},{28,24},{5,1},{9,5},{13... | collective-permute-start | bytes 589832 | tf_op jit(solution)/shard_map/ppermute | solution.py:29
  12.7 14.5 %collective-permute-start.2 = (f32[3,2,256,64]{2,3,1,0:T(8,128)S(1)}, f32[3,2,256,64]{2,3,1,0:T(8,128)S(1)}, u32[]{:S(2)}, u32[]{:S(2)}) collective-permute-start(f32[3,2,256,64]{2,3,1,0:T(8,128)S(1)} %get-tuple-element.167), channel_id=1, source_target_pairs={{0,1},{1,2},{2,3},{4,5},{5,6},{6,7},{8,9},{9,10},{10,11},{12,13},{... | collective-permute-start | bytes 1179656 | tf_op jit(solution)/shard_map/ppermute | solution.py:26
  16.1 19.1 %collective-permute-start.3 = (f32[3,2,256,64]{2,3,1,0:T(8,128)S(1)}, f32[3,2,256,64]{2,3,1,0:T(8,128)}, u32[]{:S(2)}, u32[]{:S(2)}) collective-permute-start(f32[3,2,256,64]{2,3,1,0:T(8,128)S(1)} %get-tuple-element.168), channel_id=1, source_target_pairs={{1,0},{2,1},{3,2},{5,4},{6,5},{7,6},{9,8},{10,9},{11,10},{13,12},{... | collective-permute-start | bytes 1179656 | tf_op jit(solution)/shard_map/ppermute | solution.py:29
  36.6 2.2 copy-start.2
  38.8 0.9 copy-start.3
  39.7 2.2 copy-start.2
  43.4 5.1 %copy-start.4 = (f32[2,3,2,128,128]{4,3,0,2,1:T(8,128)S(1)}, f32[2,3,2,128,128]{4,3,0,2,1:T(8,128)}, u32[]{:S(2)}) copy-start(f32[2,3,2,128,128]{4,3,0,2,1:T(8,128)} %get-tuple-element.108) | copy-start | bytes 2359300
  63.3 4.2 %copy-start = (f32[1,1,2,128,128]{4,3,2,1,0:T(8,128)S(1)}, f32[1,1,2,128,128]{4,3,2,1,0:T(8,128)}, u32[]{:S(2)}) copy-start(f32[1,1,2,128,128]{4,3,2,1,0:T(8,128)} %param.23) | copy-start | bytes 393220
  109.6 10.8 %collective-permute-start.4 = (f32[3,2,64,256]{3,2,1,0:T(8,128)S(1)}, f32[3,2,64,256]{3,2,1,0:T(8,128)S(1)}, u32[]{:S(2)}, u32[]{:S(2)}) collective-permute-start(f32[3,2,64,256]{3,2,1,0:T(8,128)S(1)} %get-tuple-element.144), channel_id=1, source_target_pairs={{4,0},{8,4},{12,8},{16,12},{20,16},{24,20},{28,24},{5,1},{9,5},{13... | collective-permute-start | bytes 1179656 | tf_op jit(solution)/shard_map/ppermute | solution.py:18
  115.0 9.1 %collective-permute-start.5 = (f32[3,2,64,256]{3,2,1,0:T(8,128)S(1)}, f32[3,2,64,256]{3,2,1,0:T(8,128)S(1)}, u32[]{:S(2)}, u32[]{:S(2)}) collective-permute-start(f32[3,2,64,256]{3,2,1,0:T(8,128)S(1)} %get-tuple-element.143), channel_id=1, source_target_pairs={{0,4},{4,8},{8,12},{12,16},{16,20},{20,24},{24,28},{1,5},{5,9},{9,... | collective-permute-start | bytes 1179656 | tf_op jit(solution)/shard_map/ppermute | solution.py:18
  124.4 14.8 %collective-permute-start.6 = (f32[3,2,128,64]{3,2,1,0:T(8,128)S(1)}, f32[3,2,128,64]{3,2,1,0:T(8,128)S(1)}, u32[]{:S(2)}, u32[]{:S(2)}) collective-permute-start(f32[3,2,128,64]{3,2,1,0:T(8,128)S(1)} %get-tuple-element.166), channel_id=1, source_target_pairs={{1,0},{2,1},{3,2},{5,4},{6,5},{7,6},{9,8},{10,9},{11,10},{13,12},{... | collective-permute-start | bytes 589832 | tf_op jit(solution)/shard_map/ppermute | solution.py:18
  127.1 16.9 %collective-permute-start.7 = (f32[3,2,128,64]{3,2,1,0:T(8,128)S(1)}, f32[3,2,128,64]{3,2,1,0:T(8,128)S(1)}, u32[]{:S(2)}, u32[]{:S(2)}) collective-permute-start(f32[3,2,128,64]{3,2,1,0:T(8,128)S(1)} %get-tuple-element.165), channel_id=1, source_target_pairs={{0,1},{1,2},{2,3},{4,5},{5,6},{6,7},{8,9},{9,10},{10,11},{12,13},{... | collective-permute-start | bytes 589832 | tf_op jit(solution)/shard_map/ppermute | solution.py:18
  139.3 8.3 %copy-start.1 = (f32[3,2,128,128]{3,2,1,0:T(8,128)S(1)}, f32[3,2,128,128]{3,2,1,0:T(8,128)}, u32[]{:S(2)}) copy-start(f32[3,2,128,128]{3,2,1,0:T(8,128)} %param.21) | copy-start | bytes 1179652
  147.7 7.0 %collective-permute-start.8 = (f32[3,2,64,128]{3,2,1,0:T(8,128)S(1)}, f32[3,2,64,128]{3,2,1,0:T(8,128)S(1)}, u32[]{:S(2)}, u32[]{:S(2)}) collective-permute-start(f32[3,2,64,128]{3,2,1,0:T(8,128)S(1)} %get-tuple-element.179), channel_id=1, source_target_pairs={{0,4},{4,8},{8,12},{12,16},{16,20},{20,24},{24,28},{1,5},{5,9},{9,... | collective-permute-start | bytes 589832 | tf_op jit(solution)/shard_map/ppermute | solution.py:26
  149.6 6.8 %collective-permute-start.9 = (f32[3,2,64,128]{3,2,1,0:T(8,128)S(1)}, f32[3,2,64,128]{3,2,1,0:T(8,128)S(1)}, u32[]{:S(2)}, u32[]{:S(2)}) collective-permute-start(f32[3,2,64,128]{3,2,1,0:T(8,128)S(1)} %get-tuple-element.180), channel_id=1, source_target_pairs={{4,0},{8,4},{12,8},{16,12},{20,16},{24,20},{28,24},{5,1},{9,5},{13... | collective-permute-start | bytes 589832 | tf_op jit(solution)/shard_map/ppermute | solution.py:29
  157.7 14.8 %collective-permute-start.10 = (f32[3,2,256,64]{2,3,1,0:T(8,128)S(1)}, f32[3,2,256,64]{2,3,1,0:T(8,128)S(1)}, u32[]{:S(2)}, u32[]{:S(2)}) collective-permute-start(f32[3,2,256,64]{2,3,1,0:T(8,128)S(1)} %copy.154), channel_id=1, source_target_pairs={{0,1},{1,2},{2,3},{4,5},{5,6},{6,7},{8,9},{9,10},{10,11},{12,13},{... | collective-permute-start | bytes 1179656 | tf_op jit(solution)/shard_map/ppermute | solution.py:26
  163.2 16.9 %collective-permute-start.11 = (f32[3,2,256,64]{2,3,1,0:T(8,128)S(1)}, f32[3,2,256,64]{2,3,1,0:T(8,128)S(1)}, u32[]{:S(2)}, u32[]{:S(2)}) collective-permute-start(f32[3,2,256,64]{2,3,1,0:T(8,128)S(1)} %copy.155), channel_id=1, source_target_pairs={{1,0},{2,1},{3,2},{5,4},{6,5},{7,6},{9,8},{10,9},{11,10},{13,12},{... | collective-permute-start | bytes 1179656 | tf_op jit(solution)/shard_map/ppermute | solution.py:29
  250.1 11.2 %collective-permute-start.12 = (f32[3,2,64,256]{3,2,1,0:T(8,128)S(1)}, f32[3,2,64,256]{3,2,1,0:T(8,128)S(1)}, u32[]{:S(2)}, u32[]{:S(2)}) collective-permute-start(f32[3,2,64,256]{3,2,1,0:T(8,128)S(1)} %get-tuple-element.142), channel_id=1, source_target_pairs={{4,0},{8,4},{12,8},{16,12},{20,16},{24,20},{28,24},{5,1},{9,5},{13... | collective-permute-start | bytes 1179656 | tf_op jit(solution)/shard_map/ppermute | solution.py:18
  256.0 9.1 %collective-permute-start.13 = (f32[3,2,64,256]{3,2,1,0:T(8,128)S(1)}, f32[3,2,64,256]{3,2,1,0:T(8,128)S(1)}, u32[]{:S(2)}, u32[]{:S(2)}) collective-permute-start(f32[3,2,64,256]{3,2,1,0:T(8,128)S(1)} %get-tuple-element.141), channel_id=1, source_target_pairs={{0,4},{4,8},{8,12},{12,16},{16,20},{20,24},{24,28},{1,5},{5,9},{9,... | collective-permute-start | bytes 1179656 | tf_op jit(solution)/shard_map/ppermute | solution.py:18
  265.4 14.0 %collective-permute-start.14 = (f32[3,2,128,64]{3,2,1,0:T(8,128)S(1)}, f32[3,2,128,64]{3,2,1,0:T(8,128)S(1)}, u32[]{:S(2)}, u32[]{:S(2)}) collective-permute-start(f32[3,2,128,64]{3,2,1,0:T(8,128)S(1)} %get-tuple-element.162), channel_id=1, source_target_pairs={{1,0},{2,1},{3,2},{5,4},{6,5},{7,6},{9,8},{10,9},{11,10},{13,12},{... | collective-permute-start | bytes 589832 | tf_op jit(solution)/shard_map/ppermute | solution.py:18
  267.5 16.6 %collective-permute-start.15 = (f32[3,2,128,64]{3,2,1,0:T(8,128)S(1)}, f32[3,2,128,64]{3,2,1,0:T(8,128)S(1)}, u32[]{:S(2)}, u32[]{:S(2)}) collective-permute-start(f32[3,2,128,64]{3,2,1,0:T(8,128)S(1)} %get-tuple-element.161), channel_id=1, source_target_pairs={{0,1},{1,2},{2,3},{4,5},{5,6},{6,7},{8,9},{9,10},{10,11},{12,13},{... | collective-permute-start | bytes 589832 | tf_op jit(solution)/shard_map/ppermute | solution.py:18
  (2 other events, 1.6 us)
where the time goes:
time: 294 us; the launch traced here: 289 us
  matrix products  87.3 us (30%)
  local copies, waits for them, and re-layouts  71.9 us (24%)
  waiting for transfers between devices  58.5 us (20%)
  starting transfers between devices  52.9 us (18%)
  between operations  10 us (3%)
  other arithmetic  7.17 us (2%)
    dot_general x80, matrix products, right_mul(): return jnp.einsum('...n,nk->...k', values, matrix, precision=PRECISE)  45.4 us
    dot_general x80, matrix products, left_mul(): return jnp.einsum('...nm,nk->...km', values, matrix, precision=PRECISE)  41.9 us
    dynamic_update_slice x4, local copies, waits for them, and re-layouts, add_window(): return lax.dynamic_update_slice(running, before + update, corner_start)  37.3 us
    ppermute x8, waiting for transfers between devices, passed_along(): return lax.ppermute(block, axis, route)  29.2 us
    ppermute x8, starting transfers between devices, passed_along(): return lax.ppermute(block, axis, route)  28.7 us
    ppermute x4, waiting for transfers between devices, padded(): lax.ppermute(lax.slice_in_dim(block, 0, width, axis=dim), axis, backward)  18 us
    ppermute x4, starting transfers between devices, padded(): lax.ppermute(lax.slice_in_dim(block, block.shape[dim] - width, None, axis...  12.5 us
    ppermute x4, starting transfers between devices, padded(): lax.ppermute(lax.slice_in_dim(block, 0, width, axis=dim), axis, backward)  11.7 us
  transfers between devices with their start and end apart: 16, of which 14 were waited for; matrix products, arithmetic and copies ran while one was open for 4% of the time, Pallas kernels for 0%

commit v1 on v0

v1 whole, which is shorter than its diff:
```python
import functools

import jax
import jax.numpy as jnp
import ml_dtypes
import numpy as np
from jax import lax
from jax.experimental import pallas as pl
from jax.experimental.pallas import tpu as pltpu
from jax.sharding import PartitionSpec as P

ITERS = 2
LEARNING_RATE = 0.02


def halves_of(matrix):
    block = np.block([[matrix.real, matrix.imag], [-matrix.imag, matrix.real]])
    block = block.astype(np.float32)
    lead = block.astype(ml_dtypes.bfloat16)
    trail = (block - lead.astype(np.float32)).astype(ml_dtypes.bfloat16)
    return np.stack([lead, trail])


def make_tables(side):
    ordinal = np.arange(side)
    fourier = np.exp(-2j * np.pi / side * (np.outer(ordinal, ordinal) % side)) / np.sqrt(side)
    frequency = (ordinal + side // 2) % side - side // 2
    phase = np.exp(-0.25j * np.pi / side * frequency * frequency)
    spread = (fourier.conj() * phase[None, :]) @ fourier
    forms = [fourier, fourier.conj(), spread, spread.conj()]
    return np.stack([halves_of(form) for form in forms])


def split(values):
    lead = values.astype(jnp.bfloat16)
    return lead, (values - lead.astype(jnp.float32)).astype(jnp.bfloat16)


def dot(left, right):
    return jnp.dot(left, right, preferred_element_type=jnp.float32)


def both_sides(waves, table, form):
    side = waves[0][0].shape[0]
    stacked = jnp.concatenate([jnp.concatenate(pair, axis=1) for pair in waves], axis=0)
    lead, trail = split(stacked)
    right = (table[form, 0], table[form, 1])
    out = dot(lead, right[0]) + dot(trail, right[0]) + dot(lead, right[1])
    count = len(waves)
    turned = jnp.concatenate(
        [
            jnp.concatenate(
                [out[w * side : (w + 1) * side, part * side : (part + 1) * side] for w in range(count)],
                axis=1,
            )
            for part in range(2)
        ],
        axis=0,
    )
    lead, trail = split(turned)
    left = (table[form ^ 1, 0], table[form ^ 1, 1])
    out = dot(left[0], lead) + dot(left[0], trail) + dot(left[1], lead)
    return [
        tuple(
            out[part * side : (part + 1) * side, w * side : (w + 1) * side] for part in range(2)
        )
        for w in range(count)
    ]


def times(a, b):
    return (a[0] * b[0] - a[1] * b[1], a[0] * b[1] + a[1] * b[0])


def conj_times(a, b):
    return (a[0] * b[0] + a[1] * b[1], a[0] * b[1] - a[1] * b[0])


def masks_of(corners, window, side):
    half = side // 2
    found = []
    for dim in range(2):
        place = lax.broadcasted_iota(jnp.int32, (side, side), dim)
        corner = corners[window * 2 + dim]
        found.append((place >= corner + half) | (place < corner - half))
    return found


def compute_kernel(tiles, probe, samples, corners, count, table, grads):
    layer_count = tiles.shape[2]
    side = tiles.shape[-1]
    slots = samples.shape[0]
    half = side // 2
    masks = [masks_of(corners, w, side) for w in range(slots)]
    waves = []
    for w in range(slots):
        shifts = [lax.rem(corners[w * 2 + dim] + half, side) for dim in range(2)]
        waves.append(
            tuple(
                pltpu.roll(pltpu.roll(probe[part], shifts[0], 0), shifts[1], 1)
                for part in range(2)
            )
        )

    def layer(w, s):
        rows, cols = masks[w]
        return tuple(
            jnp.where(
                rows,
                jnp.where(cols, tiles[1, 1, s, part], tiles[1, 0, s, part]),
                jnp.where(cols, tiles[0, 1, s, part], tiles[0, 0, s, part]),
            )
            for part in range(2)
        )

    windows = range(slots)
    incident = []
    layers = []
    for s in range(layer_count):
        incident.append(waves)
        layers.append([layer(w, s) for w in windows])
        waves = [times(layers[s][w], waves[w]) for w in windows]
        if s + 1 < layer_count:
            waves = both_sides(waves, table, 2)
    far = both_sides(waves, table, 0)
    scaled = []
    for w in windows:
        residue = far[w][0] * far[w][0] + far[w][1] * far[w][1] - samples[w]
        scaled.append((residue * far[w][0], residue * far[w][1]))
    back = both_sides(scaled, table, 1)
    for s in reversed(range(layer_count)):
        pieces = [conj_times(incident[s][w], back[w]) for w in windows]
        for part in range(2):
            totals = [[0.0, 0.0], [0.0, 0.0]]
            for w in windows:
                rows, cols = masks[w]
                value = jnp.where(w < count[0], pieces[w][part], 0.0)
                split_rows = (jnp.where(rows, 0.0, value), jnp.where(rows, value, 0.0))
                for a in range(2):
                    totals[a][0] += jnp.where(cols, 0.0, split_rows[a])
                    totals[a][1] += jnp.where(cols, split_rows[a], 0.0)
            for a in range(2):
                for b in range(2):
                    grads[a, b, s, part] = totals[a][b]
        if s > 0:
            back = both_sides(
                [conj_times(layers[s][w], back[w]) for w in windows], table, 3
            )


def shifted(block, axis, step):
    size = lax.axis_size(axis)
    route = [(i, i + step) for i in range(size) if 0 <= i + step < size]
    return lax.ppermute(block, axis, route)


def swapped(block, axis, dim, outward):
    half = block.shape[dim] // 2
    low = lax.slice_in_dim(block, 0, half, axis=dim)
    high = lax.slice_in_dim(block, half, None, axis=dim)
    return jnp.concatenate([shifted(low, axis, outward), shifted(high, axis, -outward)], axis=dim)


def shards(object_field, probe, measured, positions, counts):
    samples = measured[0, 0]
    corners = positions[0, 0].reshape(-1)
    count = counts.reshape(-1)
    table = jnp.asarray(make_tables(probe.shape[-1]))
    vmem = pl.BlockSpec(memory_space=pltpu.VMEM)
    smem = pl.BlockSpec(memory_space=pltpu.SMEM)
    current = object_field
    compute = pl.pallas_call(
        compute_kernel,
        out_shape=jax.ShapeDtypeStruct((2, 2) + object_field.shape, jnp.float32),
        in_specs=[vmem, vmem, vmem, smem, smem, vmem],
        out_specs=vmem,
        name="windows",
    )
    for _ in range(ITERS):
        wide = jnp.stack([current, swapped(current, "col", 3, -1)])
        tiles = jnp.stack([wide, swapped(wide, "row", 3, -1)])
        grads = compute(tiles, probe, samples, corners, count, table)
        folded = grads[0] + swapped(grads[1], "row", 3, 1)
        current = current - LEARNING_RATE * (folded[0] + swapped(folded[1], "col", 3, 1))
    return current


def solution(mesh):
    placed = (
        P(None, None, "row", "col"),
        P(),
        P("row", "col", None, None, None),
        P("row", "col", None, None),
        P("row", "col"),
    )
    return jax.shard_map(
        shards, mesh=mesh, in_specs=placed, out_specs=P(None, None, "row", "col"), check_vma=False
    )
```

time: 294 us -> 157 us (0.53); the launches traced: 289 us -> 155 us
  matrix products: 87.3 us -> 0 us
  local copies, waits for them, and re-layouts: 71.9 us -> 5.33 us
  waiting for transfers between devices: 58.5 us -> 82.5 us
  Pallas kernels: 0 us -> 14.5 us
  between operations: 10 us -> 0.91 us
  starting transfers between devices: 52.9 us -> 47.7 us
    dot_general x160 -> x0, matrix products: 87.3 us -> none  [the longest x80 45.4 us: right_mul(): return jnp.einsum('...n,nk->...k', values, matrix, precision=PRECISE)]
    dynamic_update_slice x4 -> x0, local copies, waits for them, and re-layouts: 37.3 us -> none  [add_window(): return lax.dynamic_update_slice(running, before + update, corner_start)]
    ppermute x16, waiting for transfers between devices: 58.5 us -> 82.5 us  [shifted(): return lax.ppermute(block, axis, route)]
    scatter-add x4 -> x0, local copies, waits for them, and re-layouts: 16.2 us -> none  [the longest x2 9.24 us: fold_cols(): interior = interior.at[:, :, :, inner_size - rim_width:].add(from_right)]
    pallas_call x0 -> x2, Pallas kernels: none -> 14.5 us  [shards(): grads = compute(tiles, probe, samples, corners, count, table)]
    gather x24 -> x0, local copies, waits for them, and re-layouts: 10.4 us -> none
    ppermute x16, starting transfers between devices: 52.9 us -> 47.7 us  [shifted(): return lax.ppermute(block, axis, route)]
    concatenate x5 -> x0, other arithmetic: 3.97 us -> none  [the longest x4 3.9 us: padded(): block = jnp.concatenate([low, block, high], axis=dim)]
  transfers between devices with their start and end apart: 16 -> 16, of which waited for: 14 -> 16; matrix products, arithmetic and copies ran while one was open for 4% -> 0% of each run, Pallas kernels for 0% -> 0%
where the time goes in v1:
time: 157 us; the launch traced here: 155 us
  waiting for transfers between devices  82.5 us (53%)
  starting transfers between devices  47.7 us (30%)
  Pallas kernels  14.5 us (9%)
  local copies, waits for them, and re-layouts  5.33 us (3%)
  other arithmetic  4.55 us (3%)
    ppermute x16, waiting for transfers between devices, shifted(): return lax.ppermute(block, axis, route)  82.5 us
    ppermute x16, starting transfers between devices, shifted(): return lax.ppermute(block, axis, route)  47.7 us
    pallas_call x2, Pallas kernels, shards(): grads = compute(tiles, probe, samples, corners, count, table)  14.5 us
  transfers between devices with their start and end apart: 16, of which 16 were waited for; matrix products, arithmetic and copies ran while one was open for 0% of the time, Pallas kernels for 0%

profile of v1, /device:TPU:18, one launch (start us, length us, event | category | flops | bytes accessed | tf_op | source)
XLA Modules:
  0.0 155.5 jit_solution(10084009484710032506)
XLA Ops:
  1.4 2.4 %collective-permute-start = (f32[3,2,128,64]{3,2,1,0:T(8,128)S(1)}, f32[3,2,128,64]{3,2,1,0:T(8,128)S(1)}, u32[]{:S(2)}, u32[]{:S(2)}) collective-permute-start(f32[3,2,128,64]{3,2,1,0:T(8,128)S(1)} %get-tuple-element.19), channel_id=1, source_target_pairs={{1,0},{2,1},{3,2},{5,4},{6,5},{7,6},{9,8},{10,9},{11,10},{13,12},{... | collective-permute-start | bytes 589832 | tf_op jit(solution)/shard_map/ppermute | solution.py:154
  3.8 4.3 %collective-permute-start.1 = (f32[3,2,128,64]{3,2,1,0:T(8,128)S(1)}, f32[3,2,128,64]{3,2,1,0:T(8,128)S(1)}, u32[]{:S(2)}, u32[]{:S(2)}) collective-permute-start(f32[3,2,128,64]{3,2,1,0:T(8,128)S(1)} %get-tuple-element.20), channel_id=1, source_target_pairs={{0,1},{1,2},{2,3},{4,5},{5,6},{6,7},{8,9},{9,10},{10,11},{12,13},{... | collective-permute-start | bytes 589832 | tf_op jit(solution)/shard_map/ppermute | solution.py:154
  8.2 8.0 %collective-permute-done = f32[3,2,128,64]{3,2,1,0:T(8,128)S(1)} collective-permute-done((f32[3,2,128,64]{3,2,1,0:T(8,128)S(1)}, f32[3,2,128,64]{3,2,1,0:T(8,128)S(1)}, u32[]{:S(2)}, u32[]{:S(2)}) %collective-permute-start) | collective-permute-done | bytes 196640 | tf_op jit(solution)/shard_map/ppermute | solution.py:154
  16.2 4.5 %collective-permute-done.1 = f32[3,2,128,64]{3,2,1,0:T(8,128)S(1)} collective-permute-done((f32[3,2,128,64]{3,2,1,0:T(8,128)S(1)}, f32[3,2,128,64]{3,2,1,0:T(8,128)S(1)}, u32[]{:S(2)}, u32[]{:S(2)}) %collective-permute-start.1) | collective-permute-done | bytes 196640 | tf_op jit(solution)/shard_map/ppermute | solution.py:154
  22.8 2.4 %collective-permute-start.3 = (f32[2,3,2,64,128]{4,3,2,1,0:T(8,128)S(1)}, f32[2,3,2,64,128]{4,3,2,1,0:T(8,128)S(1)}, u32[]{:S(2)}, u32[]{:S(2)}) collective-permute-start(f32[2,3,2,64,128]{4,3,2,1,0:T(8,128)S(1)} %get-tuple-element.12), channel_id=1, source_target_pairs={{0,4},{4,8},{8,12},{12,16},{16,20},{20,24},{24,28},{1,5},{5,9},{9,... | collective-permute-start | bytes 1179656 | tf_op jit(solution)/shard_map/ppermute | solution.py:154
  28.1 3.8 %collective-permute-done.3 = f32[2,3,2,64,128]{4,3,2,1,0:T(8,128)S(1)} collective-permute-done((f32[2,3,2,64,128]{4,3,2,1,0:T(8,128)S(1)}, f32[2,3,2,64,128]{4,3,2,1,0:T(8,128)S(1)}, u32[]{:S(2)}, u32[]{:S(2)}) %collective-permute-start.3) | collective-permute-done | bytes 393248 | tf_op jit(solution)/shard_map/ppermute | solution.py:154
  33.3 7.2 %windows.2 = f32[2,2,3,2,128,128]{5,4,3,2,1,0:T(8,128)} custom-call(f32[2,2,3,2,128,128]{5,4,3,2,1,0:T(8,128)} %pad_maximum_fusion.tiles, f32[2,128,128]{2,1,0:T(8,128)} %probe.3, f32[2,128,128]{2,1,0:T(8,128)} %bitcast.54, s32[4]{0:T(128)} %reshape_squeeze.3.corners, s32[1]{0:T(128)} %bitcast.48.count, bf16[4,2,256,256]{3,2,1,0:T(8,128)(2,1)} %constant.4.clone.table), custom_call_target="tpu_custom_call" | custom-call | tf_op jit(solution)/shard_map/windows/pallas_call | solution.py:182
  43.8 3.6 %collective-permute-start.5 = (f32[2,3,2,64,128]{4,3,2,1,0:T(8,128)S(1)}, f32[2,3,2,64,128]{4,3,2,1,0:T(8,128)S(1)}, u32[]{:S(2)}, u32[]{:S(2)}) collective-permute-start(f32[2,3,2,64,128]{4,3,2,1,0:T(8,128)S(1)} %get-tuple-element.10), channel_id=1, source_target_pairs={{4,0},{8,4},{12,8},{16,12},{20,16},{24,20},{28,24},{5,1},{9,5},{13... | collective-permute-start | bytes 1179656 | tf_op jit(solution)/shard_map/ppermute | solution.py:154
  47.5 3.5 %collective-permute-done.4 = f32[2,3,2,64,128]{4,3,2,1,0:T(8,128)S(1)} collective-permute-done((f32[2,3,2,64,128]{4,3,2,1,0:T(8,128)S(1)}, f32[2,3,2,64,128]{4,3,2,1,0:T(8,128)S(1)}, u32[]{:S(2)}, u32[]{:S(2)}) %collective-permute-start.4) | collective-permute-done | bytes 393248 | tf_op jit(solution)/shard_map/ppermute | solution.py:154
  53.0 5.3 %collective-permute-start.6 = (f32[3,2,128,64]{3,2,1,0:T(8,128)S(1)}, f32[3,2,128,64]{3,2,1,0:T(8,128)S(1)}, u32[]{:S(2)}, u32[]{:S(2)}) collective-permute-start(f32[3,2,128,64]{3,2,1,0:T(8,128)S(1)} %get-tuple-element.17), channel_id=1, source_target_pairs={{0,1},{1,2},{2,3},{4,5},{5,6},{6,7},{8,9},{9,10},{10,11},{12,13},{... | collective-permute-start | bytes 589832 | tf_op jit(solution)/shard_map/ppermute | solution.py:154
  60.3 6.7 %collective-permute-done.6 = f32[3,2,128,64]{3,2,1,0:T(8,128)S(1)} collective-permute-done((f32[3,2,128,64]{3,2,1,0:T(8,128)S(1)}, f32[3,2,128,64]{3,2,1,0:T(8,128)S(1)}, u32[]{:S(2)}, u32[]{:S(2)}) %collective-permute-start.6) | collective-permute-done | bytes 196640 | tf_op jit(solution)/shard_map/ppermute | solution.py:154
  66.9 10.4 %collective-permute-done.7 = f32[3,2,128,64]{3,2,1,0:T(8,128)S(1)} collective-permute-done((f32[3,2,128,64]{3,2,1,0:T(8,128)S(1)}, f32[3,2,128,64]{3,2,1,0:T(8,128)S(1)}, u32[]{:S(2)}, u32[]{:S(2)}) %collective-permute-start.7) | collective-permute-done | bytes 196640 | tf_op jit(solution)/shard_map/ppermute | solution.py:154
  77.7 2.4 %collective-permute-start.8 = (f32[3,2,128,64]{3,2,1,0:T(8,128)S(1)}, f32[3,2,128,64]{3,2,1,0:T(8,128)S(1)}, u32[]{:S(2)}, u32[]{:S(2)}) collective-permute-start(f32[3,2,128,64]{3,2,1,0:T(8,128)S(1)} %get-tuple-element.15), channel_id=1, source_target_pairs={{1,0},{2,1},{3,2},{5,4},{6,5},{7,6},{9,8},{10,9},{11,10},{13,12},{... | collective-permute-start | bytes 589832 | tf_op jit(solution)/shard_map/ppermute | solution.py:154
  80.1 4.3 %collective-permute-start.9 = (f32[3,2,128,64]{3,2,1,0:T(8,128)S(1)}, f32[3,2,128,64]{3,2,1,0:T(8,128)S(1)}, u32[]{:S(2)}, u32[]{:S(2)}) collective-permute-start(f32[3,2,128,64]{3,2,1,0:T(8,128)S(1)} %get-tuple-element.16), channel_id=1, source_target_pairs={{0,1},{1,2},{2,3},{4,5},{5,6},{6,7},{8,9},{9,10},{10,11},{12,13},{... | collective-permute-start | bytes 589832 | tf_op jit(solution)/shard_map/ppermute | solution.py:154
  84.4 8.0 %collective-permute-done.8 = f32[3,2,128,64]{3,2,1,0:T(8,128)S(1)} collective-permute-done((f32[3,2,128,64]{3,2,1,0:T(8,128)S(1)}, f32[3,2,128,64]{3,2,1,0:T(8,128)S(1)}, u32[]{:S(2)}, u32[]{:S(2)}) %collective-permute-start.8) | collective-permute-done | bytes 196640 | tf_op jit(solution)/shard_map/ppermute | solution.py:154
  92.5 5.3 %collective-permute-done.9 = f32[3,2,128,64]{3,2,1,0:T(8,128)S(1)} collective-permute-done((f32[3,2,128,64]{3,2,1,0:T(8,128)S(1)}, f32[3,2,128,64]{3,2,1,0:T(8,128)S(1)}, u32[]{:S(2)}, u32[]{:S(2)}) %collective-permute-start.9) | collective-permute-done | bytes 196640 | tf_op jit(solution)/shard_map/ppermute | solution.py:154
  102.4 2.8 %collective-permute-done.10 = f32[2,3,2,64,128]{4,3,2,1,0:T(8,128)S(1)} collective-permute-done((f32[2,3,2,64,128]{4,3,2,1,0:T(8,128)S(1)}, f32[2,3,2,64,128]{4,3,2,1,0:T(8,128)S(1)}, u32[]{:S(2)}, u32[]{:S(2)}) %collective-permute-start.10) | collective-permute-done | bytes 393248 | tf_op jit(solution)/shard_map/ppermute | solution.py:154
  105.2 3.8 %collective-permute-done.11 = f32[2,3,2,64,128]{4,3,2,1,0:T(8,128)S(1)} collective-permute-done((f32[2,3,2,64,128]{4,3,2,1,0:T(8,128)S(1)}, f32[2,3,2,64,128]{4,3,2,1,0:T(8,128)S(1)}, u32[]{:S(2)}, u32[]{:S(2)}) %collective-permute-start.11) | collective-permute-done | bytes 393248 | tf_op jit(solution)/shard_map/ppermute | solution.py:154
  110.4 7.2 %windows.3 = f32[2,2,3,2,128,128]{5,4,3,2,1,0:T(8,128)} custom-call(f32[2,2,3,2,128,128]{5,4,3,2,1,0:T(8,128)} %pad_maximum_fusion.1.tiles, f32[2,128,128]{2,1,0:T(8,128)} %probe.3, f32[2,128,128]{2,1,0:T(8,128)} %bitcast.55, s32[4]{0:T(128)} %reshape_squeeze.3.corners, s32[1]{0:T(128)} %bitcast.49.count, bf16[4,2,256,256]{3,2,1,0:T(8,128)(2,1)} %constant.4.clone.table), custom_call_target="tpu_custom_call" | custom-call | tf_op jit(solution)/shard_map/windows/pallas_call | solution.py:182
  120.9 3.6 %collective-permute-start.13 = (f32[2,3,2,64,128]{4,3,2,1,0:T(8,128)S(1)}, f32[2,3,2,64,128]{4,3,2,1,0:T(8,128)S(1)}, u32[]{:S(2)}, u32[]{:S(2)}) collective-permute-start(f32[2,3,2,64,128]{4,3,2,1,0:T(8,128)S(1)} %get-tuple-element.6), channel_id=1, source_target_pairs={{4,0},{8,4},{12,8},{16,12},{20,16},{24,20},{28,24},{5,1},{9,5},{13... | collective-permute-start | bytes 1179656 | tf_op jit(solution)/shard_map/ppermute | solution.py:154
  124.6 3.5 %collective-permute-done.12 = f32[2,3,2,64,128]{4,3,2,1,0:T(8,128)S(1)} collective-permute-done((f32[2,3,2,64,128]{4,3,2,1,0:T(8,128)S(1)}, f32[2,3,2,64,128]{4,3,2,1,0:T(8,128)S(1)}, u32[]{:S(2)}, u32[]{:S(2)}) %collective-permute-start.12) | collective-permute-done | bytes 393248 | tf_op jit(solution)/shard_map/ppermute | solution.py:154
  130.2 5.3 %collective-permute-start.14 = (f32[3,2,128,64]{3,2,1,0:T(8,128)S(1)}, f32[3,2,128,64]{3,2,1,0:T(8,128)S(1)}, u32[]{:S(2)}, u32[]{:S(2)}) collective-permute-start(f32[3,2,128,64]{3,2,1,0:T(8,128)S(1)} %get-tuple-element.13), channel_id=1, source_target_pairs={{0,1},{1,2},{2,3},{4,5},{5,6},{6,7},{8,9},{9,10},{10,11},{12,13},{... | collective-permute-start | bytes 589832 | tf_op jit(solution)/shard_map/ppermute | solution.py:154
  137.4 6.8 %collective-permute-done.14 = f32[3,2,128,64]{3,2,1,0:T(8,128)S(1)} collective-permute-done((f32[3,2,128,64]{3,2,1,0:T(8,128)S(1)}, f32[3,2,128,64]{3,2,1,0:T(8,128)S(1)}, u32[]{:S(2)}, u32[]{:S(2)}) %collective-permute-start.14) | collective-permute-done | bytes 196640 | tf_op jit(solution)/shard_map/ppermute | solution.py:154
  144.2 10.4 %collective-permute-done.15 = f32[3,2,128,64]{3,2,1,0:T(8,128)S(1)} collective-permute-done((f32[3,2,128,64]{3,2,1,0:T(8,128)S(1)}, f32[3,2,128,64]{3,2,1,0:T(8,128)S(1)}, u32[]{:S(2)}, u32[]{:S(2)}) %collective-permute-start.15) | collective-permute-done | bytes 196640 | tf_op jit(solution)/shard_map/ppermute | solution.py:154
  (43 shorter events, 28.9 us)
Async XLA Ops:
  0.0 20.8 %copy-start = (f32[3,2,128,128]{3,2,1,0:T(8,128)S(1)}, f32[3,2,128,128]{3,2,1,0:T(8,128)}, u32[]{:S(2)}) copy-start(f32[3,2,128,128]{3,2,1,0:T(8,128)} %param.6) | copy-start | bytes 1179652
  1.4 24.5 %copy-start.3 = (s32[1,1,2,2]{3,2,1,0:T(2,128)S(1)}, s32[1,1,2,2]{3,2,1,0:T(2,128)}, u32[]{:S(2)}) copy-start(s32[1,1,2,2]{3,2,1,0:T(2,128)} %param.9) | copy-start | bytes 52
  1.4 14.8 %collective-permute-start = (f32[3,2,128,64]{3,2,1,0:T(8,128)S(1)}, f32[3,2,128,64]{3,2,1,0:T(8,128)S(1)}, u32[]{:S(2)}, u32[]{:S(2)}) collective-permute-start(f32[3,2,128,64]{3,2,1,0:T(8,128)S(1)} %get-tuple-element.19), channel_id=1, source_target_pairs={{1,0},{2,1},{3,2},{5,4},{6,5},{7,6},{9,8},{10,9},{11,10},{13,12},{... | collective-permute-start | bytes 589832 | tf_op jit(solution)/shard_map/ppermute | solution.py:154
  3.8 16.8 %collective-permute-start.1 = (f32[3,2,128,64]{3,2,1,0:T(8,128)S(1)}, f32[3,2,128,64]{3,2,1,0:T(8,128)S(1)}, u32[]{:S(2)}, u32[]{:S(2)}) collective-permute-start(f32[3,2,128,64]{3,2,1,0:T(8,128)S(1)} %get-tuple-element.20), channel_id=1, source_target_pairs={{0,1},{1,2},{2,3},{4,5},{5,6},{6,7},{8,9},{9,10},{10,11},{12,13},{... | collective-permute-start | bytes 589832 | tf_op jit(solution)/shard_map/ppermute | solution.py:154
  20.9 7.2 %collective-permute-start.2 = (f32[2,3,2,64,128]{4,3,2,1,0:T(8,128)S(1)}, f32[2,3,2,64,128]{4,3,2,1,0:T(8,128)S(1)}, u32[]{:S(2)}, u32[]{:S(2)}) collective-permute-start(f32[2,3,2,64,128]{4,3,2,1,0:T(8,128)S(1)} %get-tuple-element.11), channel_id=1, source_target_pairs={{4,0},{8,4},{12,8},{16,12},{20,16},{24,20},{28,24},{5,1},{9,5},{13... | collective-permute-start | bytes 1179656 | tf_op jit(solution)/shard_map/ppermute | solution.py:154
  22.8 9.1 %collective-permute-start.3 = (f32[2,3,2,64,128]{4,3,2,1,0:T(8,128)S(1)}, f32[2,3,2,64,128]{4,3,2,1,0:T(8,128)S(1)}, u32[]{:S(2)}, u32[]{:S(2)}) collective-permute-start(f32[2,3,2,64,128]{4,3,2,1,0:T(8,128)S(1)} %get-tuple-element.12), channel_id=1, source_target_pairs={{0,4},{4,8},{8,12},{12,16},{16,20},{20,24},{24,28},{1,5},{5,9},{9,... | collective-permute-start | bytes 1179656 | tf_op jit(solution)/shard_map/ppermute | solution.py:154
  40.5 12.2 %copy-start.2 = (f32[2,2,3,2,128,128]{5,4,3,2,1,0:T(8,128)S(1)}, f32[2,2,3,2,128,128]{5,4,3,2,1,0:T(8,128)}, u32[]{:S(2)}) copy-start(f32[2,2,3,2,128,128]{5,4,3,2,1,0:T(8,128)} %windows.2) | copy-start | bytes 4718596
  41.9 9.1 %collective-permute-start.4 = (f32[2,3,2,64,128]{4,3,2,1,0:T(8,128)S(1)}, f32[2,3,2,64,128]{4,3,2,1,0:T(8,128)S(1)}, u32[]{:S(2)}, u32[]{:S(2)}) collective-permute-start(f32[2,3,2,64,128]{4,3,2,1,0:T(8,128)S(1)} %get-tuple-element.9), channel_id=1, source_target_pairs={{0,4},{4,8},{8,12},{12,16},{16,20},{20,24},{24,28},{1,5},{5,9},{9,... | collective-permute-start | bytes 1179656 | tf_op jit(solution)/shard_map/ppermute | solution.py:154
  43.8 8.9 %collective-permute-start.5 = (f32[2,3,2,64,128]{4,3,2,1,0:T(8,128)S(1)}, f32[2,3,2,64,128]{4,3,2,1,0:T(8,128)S(1)}, u32[]{:S(2)}, u32[]{:S(2)}) collective-permute-start(f32[2,3,2,64,128]{4,3,2,1,0:T(8,128)S(1)} %get-tuple-element.10), channel_id=1, source_target_pairs={{4,0},{8,4},{12,8},{16,12},{20,16},{24,20},{28,24},{5,1},{9,5},{13... | collective-permute-start | bytes 1179656 | tf_op jit(solution)/shard_map/ppermute | solution.py:154
  53.0 13.9 %collective-permute-start.6 = (f32[3,2,128,64]{3,2,1,0:T(8,128)S(1)}, f32[3,2,128,64]{3,2,1,0:T(8,128)S(1)}, u32[]{:S(2)}, u32[]{:S(2)}) collective-permute-start(f32[3,2,128,64]{3,2,1,0:T(8,128)S(1)} %get-tuple-element.17), channel_id=1, source_target_pairs={{0,1},{1,2},{2,3},{4,5},{5,6},{6,7},{8,9},{9,10},{10,11},{12,13},{... | collective-permute-start | bytes 589832 | tf_op jit(solution)/shard_map/ppermute | solution.py:154
  58.3 19.0 %collective-permute-start.7 = (f32[3,2,128,64]{3,2,1,0:T(8,128)S(1)}, f32[3,2,128,64]{3,2,1,0:T(8,128)S(1)}, u32[]{:S(2)}, u32[]{:S(2)}) collective-permute-start(f32[3,2,128,64]{3,2,1,0:T(8,128)S(1)} %get-tuple-element.18), channel_id=1, source_target_pairs={{1,0},{2,1},{3,2},{5,4},{6,5},{7,6},{9,8},{10,9},{11,10},{13,12},{... | collective-permute-start | bytes 589832 | tf_op jit(solution)/shard_map/ppermute | solution.py:154
  77.7 14.8 %collective-permute-start.8 = (f32[3,2,128,64]{3,2,1,0:T(8,128)S(1)}, f32[3,2,128,64]{3,2,1,0:T(8,128)S(1)}, u32[]{:S(2)}, u32[]{:S(2)}) collective-permute-start(f32[3,2,128,64]{3,2,1,0:T(8,128)S(1)} %get-tuple-element.15), channel_id=1, source_target_pairs={{1,0},{2,1},{3,2},{5,4},{6,5},{7,6},{9,8},{10,9},{11,10},{13,12},{... | collective-permute-start | bytes 589832 | tf_op jit(solution)/shard_map/ppermute | solution.py:154
  80.1 17.6 %collective-permute-start.9 = (f32[3,2,128,64]{3,2,1,0:T(8,128)S(1)}, f32[3,2,128,64]{3,2,1,0:T(8,128)S(1)}, u32[]{:S(2)}, u32[]{:S(2)}) collective-permute-start(f32[3,2,128,64]{3,2,1,0:T(8,128)S(1)} %get-tuple-element.16), channel_id=1, source_target_pairs={{0,1},{1,2},{2,3},{4,5},{5,6},{6,7},{8,9},{9,10},{10,11},{12,13},{... | collective-permute-start | bytes 589832 | tf_op jit(solution)/shard_map/ppermute | solution.py:154
  98.0 7.2 %collective-permute-start.10 = (f32[2,3,2,64,128]{4,3,2,1,0:T(8,128)S(1)}, f32[2,3,2,64,128]{4,3,2,1,0:T(8,128)S(1)}, u32[]{:S(2)}, u32[]{:S(2)}) collective-permute-start(f32[2,3,2,64,128]{4,3,2,1,0:T(8,128)S(1)} %get-tuple-element.7), channel_id=1, source_target_pairs={{4,0},{8,4},{12,8},{16,12},{20,16},{24,20},{28,24},{5,1},{9,5},{13... | collective-permute-start | bytes 1179656 | tf_op jit(solution)/shard_map/ppermute | solution.py:154
  100.0 9.1 %collective-permute-start.11 = (f32[2,3,2,64,128]{4,3,2,1,0:T(8,128)S(1)}, f32[2,3,2,64,128]{4,3,2,1,0:T(8,128)S(1)}, u32[]{:S(2)}, u32[]{:S(2)}) collective-permute-start(f32[2,3,2,64,128]{4,3,2,1,0:T(8,128)S(1)} %get-tuple-element.8), channel_id=1, source_target_pairs={{0,4},{4,8},{8,12},{12,16},{16,20},{20,24},{24,28},{1,5},{5,9},{9,... | collective-permute-start | bytes 1179656 | tf_op jit(solution)/shard_map/ppermute | solution.py:154
  117.6 12.2 %copy-start.1 = (f32[2,2,3,2,128,128]{5,4,3,2,1,0:T(8,128)S(1)}, f32[2,2,3,2,128,128]{5,4,3,2,1,0:T(8,128)}, u32[]{:S(2)}) copy-start(f32[2,2,3,2,128,128]{5,4,3,2,1,0:T(8,128)} %windows.3) | copy-start | bytes 4718596
  119.0 9.1 %collective-permute-start.12 = (f32[2,3,2,64,128]{4,3,2,1,0:T(8,128)S(1)}, f32[2,3,2,64,128]{4,3,2,1,0:T(8,128)S(1)}, u32[]{:S(2)}, u32[]{:S(2)}) collective-permute-start(f32[2,3,2,64,128]{4,3,2,1,0:T(8,128)S(1)} %get-tuple-element.5), channel_id=1, source_target_pairs={{0,4},{4,8},{8,12},{12,16},{16,20},{20,24},{24,28},{1,5},{5,9},{9,... | collective-permute-start | bytes 1179656 | tf_op jit(solution)/shard_map/ppermute | solution.py:154
  120.9 8.9 %collective-permute-start.13 = (f32[2,3,2,64,128]{4,3,2,1,0:T(8,128)S(1)}, f32[2,3,2,64,128]{4,3,2,1,0:T(8,128)S(1)}, u32[]{:S(2)}, u32[]{:S(2)}) collective-permute-start(f32[2,3,2,64,128]{4,3,2,1,0:T(8,128)S(1)} %get-tuple-element.6), channel_id=1, source_target_pairs={{4,0},{8,4},{12,8},{16,12},{20,16},{24,20},{28,24},{5,1},{9,5},{13... | collective-permute-start | bytes 1179656 | tf_op jit(solution)/shard_map/ppermute | solution.py:154
  130.2 14.0 %collective-permute-start.14 = (f32[3,2,128,64]{3,2,1,0:T(8,128)S(1)}, f32[3,2,128,64]{3,2,1,0:T(8,128)S(1)}, u32[]{:S(2)}, u32[]{:S(2)}) collective-permute-start(f32[3,2,128,64]{3,2,1,0:T(8,128)S(1)} %get-tuple-element.13), channel_id=1, source_target_pairs={{0,1},{1,2},{2,3},{4,5},{5,6},{6,7},{8,9},{9,10},{10,11},{12,13},{... | collective-permute-start | bytes 589832 | tf_op jit(solution)/shard_map/ppermute | solution.py:154
  135.5 19.1 %collective-permute-start.15 = (f32[3,2,128,64]{3,2,1,0:T(8,128)S(1)}, f32[3,2,128,64]{3,2,1,0:T(8,128)S(1)}, u32[]{:S(2)}, u32[]{:S(2)}) collective-permute-start(f32[3,2,128,64]{3,2,1,0:T(8,128)S(1)} %get-tuple-element.14), channel_id=1, source_target_pairs={{1,0},{2,1},{3,2},{5,4},{6,5},{7,6},{9,8},{10,9},{11,10},{13,12},{... | collective-permute-start | bytes 589832 | tf_op jit(solution)/shard_map/ppermute | solution.py:154

commit v2 on v1

v2 whole, which is shorter than its diff:
```python
import functools

import jax
import jax.numpy as jnp
import ml_dtypes
import numpy as np
from jax import lax
from jax.experimental import pallas as pl
from jax.experimental.pallas import tpu as pltpu
from jax.sharding import PartitionSpec as P

ITERS = 2
LEARNING_RATE = 0.02


def halves_of(matrix):
    block = np.block([[matrix.real, matrix.imag], [-matrix.imag, matrix.real]])
    block = block.astype(np.float32)
    lead = block.astype(ml_dtypes.bfloat16)
    trail = (block - lead.astype(np.float32)).astype(ml_dtypes.bfloat16)
    return np.stack([lead, trail])


def make_tables(side):
    ordinal = np.arange(side)
    fourier = np.exp(-2j * np.pi / side * (np.outer(ordinal, ordinal) % side)) / np.sqrt(side)
    frequency = (ordinal + side // 2) % side - side // 2
    phase = np.exp(-0.25j * np.pi / side * frequency * frequency)
    spread = (fourier.conj() * phase[None, :]) @ fourier
    forms = [fourier, fourier.conj(), spread, spread.conj()]
    return np.stack([halves_of(form) for form in forms])


def split(values):
    lead = values.astype(jnp.bfloat16)
    return lead, (values - lead.astype(jnp.float32)).astype(jnp.bfloat16)


def dot(left, right):
    return jnp.dot(left, right, preferred_element_type=jnp.float32)


def both_sides(waves, table, form):
    side = waves[0][0].shape[0]
    stacked = jnp.concatenate([jnp.concatenate(pair, axis=1) for pair in waves], axis=0)
    lead, trail = split(stacked)
    right = (table[form, 0], table[form, 1])
    out = dot(lead, right[0]) + dot(trail, right[0]) + dot(lead, right[1])
    count = len(waves)
    turned = jnp.concatenate(
        [
            jnp.concatenate(
                [out[w * side : (w + 1) * side, part * side : (part + 1) * side] for w in range(count)],
                axis=1,
            )
            for part in range(2)
        ],
        axis=0,
    )
    lead, trail = split(turned)
    left = (table[form ^ 1, 0], table[form ^ 1, 1])
    out = dot(left[0], lead) + dot(left[0], trail) + dot(left[1], lead)
    return [
        tuple(
            out[part * side : (part + 1) * side, w * side : (w + 1) * side] for part in range(2)
        )
        for w in range(count)
    ]


def times(a, b):
    return (a[0] * b[0] - a[1] * b[1], a[0] * b[1] + a[1] * b[0])


def conj_times(a, b):
    return (a[0] * b[0] + a[1] * b[1], a[0] * b[1] - a[1] * b[0])


def masks_of(corners, window, side):
    half = side // 2
    found = []
    for dim in range(2):
        place = lax.broadcasted_iota(jnp.int32, (side, side), dim)
        corner = corners[window * 2 + dim]
        found.append((place >= corner + half) | (place < corner - half))
    return found


def pack(tile):
    half = tile.shape[0] // 2
    lane = lax.broadcasted_iota(jnp.int32, (half, tile.shape[1]), 1)
    low, high = tile[:half], tile[half:]
    left = jnp.where(lane < half, low, pltpu.roll(high, half, 1))
    right = jnp.where(lane < half, pltpu.roll(low, half, 1), high)
    return left, right


def unpack(left, right):
    half = left.shape[0]
    lane = lax.broadcasted_iota(jnp.int32, left.shape, 1)
    low = jnp.where(lane < half, left, pltpu.roll(right, half, 1))
    high = jnp.where(lane < half, pltpu.roll(left, half, 1), right)
    return jnp.concatenate([low, high], axis=0)


PHASES = ("tall", "wide", "corner", "fold_rows", "fold_cols")


def step_kernel(
    shape, field, probe, samples, corners, count, table_far, out,
    table, later, vert, horz, diag, halo_out, halo_in, grad_rows, grad_in, grad_cols, fold_in,
    kept, send_sem, recv_sem, table_sem,
):
    layer_count = field.shape[0]
    side = field.shape[-1]
    slots = samples.shape[0]
    half = side // 2
    windows = range(slots)
    slices = range(layer_count)
    me = {axis: lax.axis_index(axis) for axis in shape}
    has = {axis: (me[axis] > 0, me[axis] < shape[axis] - 1) for axis in shape}
    own = [field] + [later.at[t] for t in range(ITERS - 1)]
    parts = (pl.ds(0, half), pl.ds(half, half))

    def copy(phase, t, s, d):
        if phase == "tall":
            axis, src, dst = "row", own[t].at[s, :, parts[d]], vert.at[t, s, :, parts[d]]
        elif phase == "wide":
            axis, src, dst = "col", halo_out.at[t, d, s], halo_in.at[t, d, s]
        elif phase == "corner":
            axis, src, dst = "row", horz.at[t, s, :, parts[d]], diag.at[t, s, :, parts[d]]
        elif phase == "fold_rows":
            rows = parts[1 - d]
            axis, src, dst = "row", grad_rows.at[t, s, :, :, rows], grad_in.at[t, s, :, :, rows]
        else:
            axis, src, dst = "col", grad_cols.at[t, 1 - d, s], fold_in.at[t, 1 - d, s]
        number = PHASES.index(phase)
        return axis, dst, pltpu.make_async_remote_copy(
            src_ref=src,
            dst_ref=dst,
            send_sem=send_sem.at[t, number, s, d],
            recv_sem=recv_sem.at[t, number, s, d],
            device_id={axis: me[axis] + (1 if d else -1)},
            device_id_type=pl.DeviceIdType.MESH,
        )

    def start(phase, t, s):
        for d in range(2):
            axis, _, moved = copy(phase, t, s, d)
            pl.when(has[axis][d])(moved.start)

    def arrive(phase, t, s):
        for d in range(2):
            axis, _, moved = copy(phase, t, s, d)
            pl.when(has[axis][1 - d])(moved.wait_recv)

    def uses():
        for t in range(ITERS):
            for phase in PHASES:
                for s in slices:
                    for d in range(2):
                        yield copy(phase, t, s, d) + (d,)

    load = pltpu.make_async_copy(table_far, table, table_sem)
    load.start()
    barrier = pltpu.get_barrier_semaphore()
    for axis in shape:
        for d in range(2):

            @pl.when(has[axis][d])
            def greet():
                pl.semaphore_signal(
                    barrier,
                    inc=1,
                    device_id={axis: me[axis] + (1 if d else -1)},
                    device_id_type=pl.DeviceIdType.MESH,
                )

    def ship_wide(t, s):
        for part in range(2):
            for d, piece in enumerate(pack(own[t][s, part])):
                halo_out[t, d, s, part] = piece
        start("wide", t, s)

    def ship_corner(t, s):
        arrive("wide", t, s)
        for part in range(2):
            horz[t, s, part] = unpack(halo_in[t, 0, s, part], halo_in[t, 1, s, part])
        start("corner", t, s)

    peers = sum(there.astype(jnp.int32) for axis in shape for there in has[axis])
    pl.semaphore_wait(barrier, peers)
    for s in slices:
        start("tall", 0, s)
        ship_wide(0, s)
    for axis, dst, _, d in uses():

        @pl.when(jnp.logical_not(has[axis][1 - d]))
        def clear():
            dst[...] = jnp.zeros(dst.shape, jnp.float32)

    masks = [masks_of(corners, w, side) for w in windows]
    beams = []
    for w in windows:
        shifts = [lax.rem(corners[w * 2 + dim] + half, side) for dim in range(2)]
        beams.append(
            tuple(
                pltpu.roll(pltpu.roll(probe[part], shifts[0], 0), shifts[1], 1)
                for part in range(2)
            )
        )
    load.wait()

    def layer(t, s, w):
        rows, cols = masks[w]
        return tuple(
            jnp.where(
                rows,
                jnp.where(cols, diag[t, s, part], vert[t, s, part]),
                jnp.where(cols, horz[t, s, part], own[t][s, part]),
            )
            for part in range(2)
        )

    def gather_grads(t, s, pieces):
        for part in range(2):
            totals = [[0.0, 0.0], [0.0, 0.0]]
            for w in windows:
                rows, cols = masks[w]
                value = jnp.where(w < count[0], pieces[w][part], 0.0)
                by_rows = (jnp.where(rows, 0.0, value), jnp.where(rows, value, 0.0))
                for a in range(2):
                    totals[a][0] += jnp.where(cols, 0.0, by_rows[a])
                    totals[a][1] += jnp.where(cols, by_rows[a], 0.0)
            for b in range(2):
                kept[b, s, part] = totals[0][b]
                grad_rows[t, s, b, part] = totals[1][b]
        start("fold_rows", t, s)

    def ship_cols(t, s):
        arrive("fold_rows", t, s)
        for part in range(2):
            aside = kept[1, s, part] + grad_in[t, s, 1, part]
            for d, piece in enumerate(pack(aside)):
                grad_cols[t, d, s, part] = piece
        start("fold_cols", t, s)

    def update(t, s, target):
        arrive("fold_cols", t, s)
        for part in range(2):
            inner = kept[0, s, part] + grad_in[t, s, 0, part]
            total = inner + unpack(fold_in[t, 0, s, part], fold_in[t, 1, s, part])
            target[s, part] = own[t][s, part] - LEARNING_RATE * total

    for t in range(ITERS):
        if t > 0:
            for s in slices:
                start("tall", t, s)
                ship_wide(t, s)
        waves = beams
        incident, layers = [], []
        ship_corner(t, 0)
        for s in slices:
            if s + 1 < layer_count:
                ship_corner(t, s + 1)
            arrive("tall", t, s)
            arrive("corner", t, s)
            incident.append(waves)
            layers.append([layer(t, s, w) for w in windows])
            waves = [times(layers[s][w], waves[w]) for w in windows]
            if s + 1 < layer_count:
                waves = both_sides(waves, table, 2)
        far = both_sides(waves, table, 0)
        scaled = []
        for w in windows:
            residue = far[w][0] * far[w][0] + far[w][1] * far[w][1] - samples[w]
            scaled.append((residue * far[w][0], residue * far[w][1]))
        back = both_sides(scaled, table, 1)
        for s in reversed(slices):
            gather_grads(t, s, [conj_times(incident[s][w], back[w]) for w in windows])
            if s + 1 < layer_count:
                ship_cols(t, s + 1)
            if s > 0:
                back = both_sides(
                    [conj_times(layers[s][w], back[w]) for w in windows], table, 3
                )
        ship_cols(t, 0)
        for s in reversed(slices):
            update(t, s, out if t + 1 == ITERS else own[t + 1])
    for axis, _, moved, d in uses():
        pl.when(has[axis][d])(moved.wait_send)


def shards(shape, object_field, probe, measured, positions, counts):
    samples = measured[0, 0]
    corners = positions[0, 0].reshape(-1)
    count = counts.reshape(-1)
    tables = make_tables(probe.shape[-1])
    vmem = pl.BlockSpec(memory_space=pltpu.VMEM)
    smem = pl.BlockSpec(memory_space=pltpu.SMEM)
    layer_count, _, side, _ = object_field.shape
    tiles = (layer_count, 2, side, side)
    packed = (ITERS, 2, layer_count, 2, side // 2, side)
    shapes = [
        (ITERS - 1,) + tiles,
        (ITERS,) + tiles,
        (ITERS,) + tiles,
        (ITERS,) + tiles,
        packed,
        packed,
        (ITERS, layer_count, 2, 2, side, side),
        (ITERS, layer_count, 2, 2, side, side),
        packed,
        packed,
        (2,) + tiles,
    ]
    sems = (ITERS, len(PHASES), layer_count, 2)
    return pl.pallas_call(
        functools.partial(step_kernel, shape),
        out_shape=jax.ShapeDtypeStruct(object_field.shape, jnp.float32),
        in_specs=[vmem, vmem, vmem, smem, smem, pl.BlockSpec(memory_space=pltpu.HBM)],
        out_specs=vmem,
        scratch_shapes=[pltpu.VMEM(tables.shape, jnp.bfloat16)]
        + [pltpu.VMEM(size, jnp.float32) for size in shapes]
        + [
            pltpu.SemaphoreType.DMA(sems),
            pltpu.SemaphoreType.DMA(sems),
            pltpu.SemaphoreType.DMA,
        ],
        compiler_params=pltpu.CompilerParams(collective_id=0, has_side_effects=True),
        name="steps",
    )(object_field, probe, samples, corners, count, jnp.asarray(tables))


def solution(mesh):
    placed = (
        P(None, None, "row", "col"),
        P(),
        P("row", "col", None, None, None),
        P("row", "col", None, None),
        P("row", "col"),
    )
    return jax.shard_map(
        functools.partial(shards, dict(mesh.shape)),
        mesh=mesh,
        in_specs=placed,
        out_specs=P(None, None, "row", "col"),
        check_vma=False,
    )
```

time: 157 us -> 65.9 us (0.42)
  the two profiles are of different devices: /device:TPU:18 before, /device:TPU:15 now
where the time goes in v2:
time: 65.9 us; the launch traced here: 65.7 us
  Pallas kernels  62 us (94%)
  local copies, waits for them, and re-layouts  3.03 us (5%)
  between operations  0.67 us (1%)
    pallas_call x1, Pallas kernels, shards(): pl.pallas_call(functools.partial(step_kernel, shape), out_shape=jax.Shape...  62 us
    unnamed x3, local copies, waits for them, and re-layouts  2.44 us

profile of v2, /device:TPU:15, one launch (start us, length us, event | category | flops | bytes accessed | tf_op | source)
XLA Modules:
  0.0 65.7 jit_solution(16742169913420734655)
XLA Ops:
  0.7 0.0 copy-start
  0.7 0.7 %copy-done = s32[1,1,2,2]{3,2,1,0:T(2,128)S(1)} copy-done((s32[1,1,2,2]{3,2,1,0:T(2,128)S(1)}, s32[1,1,2,2]{3,2,1,0:T(2,128)}, u32[]{:S(2)}) %copy-start) | copy-done | bytes 40
  1.3 0.6 reshape_squeeze.3.corners
  1.9 62.0 %steps.1 = f32[3,2,128,128]{3,2,1,0:T(8,128)} custom-call(f32[3,2,128,128]{3,2,1,0:T(8,128)} %field.1, f32[2,128,128]{2,1,0:T(8,128)} %probe.1, f32[2,128,128]{2,1,0:T(8,128)} %bitcast.3, s32[4]{0:T(128)} %reshape_squeeze.3.corners, s32[1]{0:T(128)} %bitcast.2.count, bf16[4,2,256,256]{3,2,1,0:T(8,128)(2,1)} %constant.2.clone.table_far), custom_call_target="tpu_custom_call" | custom-call | tf_op jit(solution)/shard_map/steps/pallas_call | solution.py:318
  64.0 1.8 %copy.9 = f32[3,2,128,128]{3,2,1,0:T(8,128)} copy(f32[3,2,128,128]{3,2,1,0:T(8,128)} %steps.1) | data formatting | bytes 786432
Async XLA Ops:
  0.7 0.7 %copy-start = (s32[1,1,2,2]{3,2,1,0:T(2,128)S(1)}, s32[1,1,2,2]{3,2,1,0:T(2,128)}, u32[]{:S(2)}) copy-start(s32[1,1,2,2]{3,2,1,0:T(2,128)} %param.9) | copy-start | bytes 52

commit v3 on v2

--- a/solution.py
+++ b/solution.py
@@ -81,7 +81,7 @@
     found = []
     for dim in range(2):
         place = lax.broadcasted_iota(jnp.int32, (side, side), dim)
-        corner = corners[window * 2 + dim]
+        corner = corners[0, 0, window, dim]
         found.append((place >= corner + half) | (place < corner - half))
     return found
 
@@ -103,13 +103,14 @@
     return jnp.concatenate([low, high], axis=0)
 
 
-PHASES = ("tall", "wide", "corner", "fold_rows", "fold_cols")
+PHASES = ("tall", "wide0", "wide1", "corner", "fold_rows", "fold_cols0", "fold_cols1")
+RELAYED = ("wide1", "fold_cols1")
 
 
 def step_kernel(
     shape, field, probe, samples, corners, count, table_far, out,
     table, later, vert, horz, diag, halo_out, halo_in, grad_rows, grad_in, grad_cols, fold_in,
-    kept, send_sem, recv_sem, table_sem,
+    kept, relay, relay_send, relay_recv, pass_send, send_sem, recv_sem, table_sem,
 ):
     layer_count = field.shape[0]
     side = field.shape[-1]
@@ -121,33 +122,67 @@
     has = {axis: (me[axis] > 0, me[axis] < shape[axis] - 1) for axis in shape}
     own = [field] + [later.at[t] for t in range(ITERS - 1)]
     parts = (pl.ds(0, half), pl.ds(half, half))
-
-    def copy(phase, t, s, d):
+    detour = shape["col"] == 4
+
+    def turns(phase, d):
+        return (me["col"] == 2 - d) if detour and phase in RELAYED else None
+
+    def both(here, phase, d):
+        away = turns(phase, d)
+        return here if away is None else jnp.logical_and(here, jnp.logical_not(away))
+
+    def copy(phase, t, s, d, leg=0):
         if phase == "tall":
             axis, src, dst = "row", own[t].at[s, :, parts[d]], vert.at[t, s, :, parts[d]]
-        elif phase == "wide":
-            axis, src, dst = "col", halo_out.at[t, d, s], halo_in.at[t, d, s]
+        elif phase.startswith("wide"):
+            part = int(phase[-1])
+            axis, src, dst = "col", halo_out.at[t, d, s, part], halo_in.at[t, d, s, part]
         elif phase == "corner":
             axis, src, dst = "row", horz.at[t, s, :, parts[d]], diag.at[t, s, :, parts[d]]
         elif phase == "fold_rows":
             rows = parts[1 - d]
             axis, src, dst = "row", grad_rows.at[t, s, :, :, rows], grad_in.at[t, s, :, :, rows]
         else:
-            axis, src, dst = "col", grad_cols.at[t, 1 - d, s], fold_in.at[t, 1 - d, s]
+            part = int(phase[-1])
+            axis, src = "col", grad_cols.at[t, 1 - d, s, part]
+            dst = fold_in.at[t, 1 - d, s, part]
         number = PHASES.index(phase)
-        return axis, dst, pltpu.make_async_remote_copy(
-            src_ref=src,
-            dst_ref=dst,
-            send_sem=send_sem.at[t, number, s, d],
-            recv_sem=recv_sem.at[t, number, s, d],
-            device_id={axis: me[axis] + (1 if d else -1)},
-            device_id_type=pl.DeviceIdType.MESH,
-        )
+        step = 1 if d else -1
+
+        def moved(src, dst, sent, landed, step):
+            return pltpu.make_async_remote_copy(
+                src_ref=src,
+                dst_ref=dst,
+                send_sem=sent,
+                recv_sem=landed,
+                device_id={axis: me[axis] + step},
+                device_id_type=pl.DeviceIdType.MESH,
+            )
+
+        landed = recv_sem.at[t, number, s, d]
+        if leg == 0:
+            return axis, dst, moved(src, dst, send_sem.at[t, number, s, d], landed, step)
+        slot = (t, RELAYED.index(phase), s)
+        if leg == 1:
+            held = relay.at[slot]
+            return axis, held, moved(src, held, relay_send.at[slot], relay_recv.at[slot], 2 * step)
+        return axis, dst, moved(relay.at[slot], dst, pass_send.at[slot], landed, -step)
 
     def start(phase, t, s):
         for d in range(2):
             axis, _, moved = copy(phase, t, s, d)
-            pl.when(has[axis][d])(moved.start)
+            pl.when(both(has[axis][d], phase, d))(moved.start)
+            if turns(phase, d) is not None:
+                pl.when(turns(phase, d))(copy(phase, t, s, d, 1)[2].start)
+
+    def hand_on(phase, t, s):
+        for d in range(2):
+            if turns(phase, d) is not None:
+
+                @pl.when(me["col"] == (3 if d else 0))
+                def forward():
+                    copy(phase, t, s, d, 1)[2].wait_recv()
+                    copy(phase, t, s, d, 2)[2].start()
 
     def arrive(phase, t, s):
         for d in range(2):
@@ -159,7 +194,7 @@
             for phase in PHASES:
                 for s in slices:
                     for d in range(2):
-                        yield copy(phase, t, s, d) + (d,)
+                        yield copy(phase, t, s, d) + (phase, d)
 
     load = pltpu.make_async_copy(table_far, table, table_sem)
     load.start()
@@ -176,24 +211,37 @@
                     device_id_type=pl.DeviceIdType.MESH,
                 )
 
+    if detour:
+        pl.semaphore_signal(
+            barrier,
+            inc=1,
+            device_id={"col": lax.rem(me["col"] + 2, shape["col"])},
+            device_id_type=pl.DeviceIdType.MESH,
+        )
+
     def ship_wide(t, s):
         for part in range(2):
             for d, piece in enumerate(pack(own[t][s, part])):
                 halo_out[t, d, s, part] = piece
-        start("wide", t, s)
+        start("wide1", t, s)
+        start("wide0", t, s)
 
     def ship_corner(t, s):
-        arrive("wide", t, s)
+        arrive("wide0", t, s)
+        arrive("wide1", t, s)
         for part in range(2):
             horz[t, s, part] = unpack(halo_in[t, 0, s, part], halo_in[t, 1, s, part])
         start("corner", t, s)
 
     peers = sum(there.astype(jnp.int32) for axis in shape for there in has[axis])
-    pl.semaphore_wait(barrier, peers)
+    pl.semaphore_wait(barrier, peers + (1 if detour else 0))
     for s in slices:
         start("tall", 0, s)
         ship_wide(0, s)
-    for axis, dst, _, d in uses():
+        if s > 0:
+            hand_on("wide1", 0, s - 1)
+    hand_on("wide1", 0, layer_count - 1)
+    for axis, dst, _, _, d in uses():
 
         @pl.when(jnp.logical_not(has[axis][1 - d]))
         def clear():
@@ -202,7 +250,7 @@
     masks = [masks_of(corners, w, side) for w in windows]
     beams = []
     for w in windows:
-        shifts = [lax.rem(corners[w * 2 + dim] + half, side) for dim in range(2)]
+        shifts = [lax.rem(corners[0, 0, w, dim] + half, side) for dim in range(2)]
         beams.append(
             tuple(
                 pltpu.roll(pltpu.roll(probe[part], shifts[0], 0), shifts[1], 1)
@@ -227,7 +275,7 @@
             totals = [[0.0, 0.0], [0.0, 0.0]]
             for w in windows:
                 rows, cols = masks[w]
-                value = jnp.where(w < count[0], pieces[w][part], 0.0)
+                value = jnp.where(w < count[0, 0], pieces[w][part], 0.0)
                 by_rows = (jnp.where(rows, 0.0, value), jnp.where(rows, value, 0.0))
                 for a in range(2):
                     totals[a][0] += jnp.where(cols, 0.0, by_rows[a])
@@ -243,10 +291,12 @@
             aside = kept[1, s, part] + grad_in[t, s, 1, part]
             for d, piece in enumerate(pack(aside)):
                 grad_cols[t, d, s, part] = piece
-        start("fold_cols", t, s)
+        start("fold_cols1", t, s)
+        start("fold_cols0", t, s)
 
     def update(t, s, target):
-        arrive("fold_cols", t, s)
+        arrive("fold_cols0", t, s)
+        arrive("fold_cols1", t, s)
         for part in range(2):
             inner = kept[0, s, part] + grad_in[t, s, 0, part]
             total = inner + unpack(fold_in[t, 0, s, part], fold_in[t, 1, s, part])
@@ -257,6 +307,9 @@
             for s in slices:
                 start("tall", t, s)
                 ship_wide(t, s)
+                if s > 0:
+                    hand_on("wide1", t, s - 1)
+            hand_on("wide1", t, layer_count - 1)
         waves = beams
         incident, layers = [], []
         ship_corner(t, 0)
@@ -280,21 +333,30 @@
             gather_grads(t, s, [conj_times(incident[s][w], back[w]) for w in windows])
             if s + 1 < layer_count:
                 ship_cols(t, s + 1)
+            if s + 2 < layer_count:
+                hand_on("fold_cols1", t, s + 2)
             if s > 0:
                 back = both_sides(
                     [conj_times(layers[s][w], back[w]) for w in windows], table, 3
                 )
         ship_cols(t, 0)
+        for s in reversed(range(min(2, layer_count))):
+            hand_on("fold_cols1", t, s)
         for s in reversed(slices):
             update(t, s, out if t + 1 == ITERS else own[t + 1])
-    for axis, _, moved, d in uses():
-        pl.when(has[axis][d])(moved.wait_send)
+    for axis, _, moved, phase, d in uses():
+        pl.when(both(has[axis][d], phase, d))(moved.wait_send)
+    for t in range(ITERS):
+        for phase in RELAYED:
+            for s in slices:
+                for d in range(2):
+                    if turns(phase, d) is not None:
+                        pl.when(turns(phase, d))(copy(phase, t, s, d, 1)[2].wait_send)
+                        pl.when(me["col"] == (3 if d else 0))(copy(phase, t, s, d, 2)[2].wait_send)
 
 
 def shards(shape, object_field, probe, measured, positions, counts):
     samples = measured[0, 0]
-    corners = positions[0, 0].reshape(-1)
-    count = counts.reshape(-1)
     tables = make_tables(probe.shape[-1])
     vmem = pl.BlockSpec(memory_space=pltpu.VMEM)
     smem = pl.BlockSpec(memory_space=pltpu.SMEM)
@@ -313,7 +375,9 @@
         packed,
         packed,
         (2,) + tiles,
+        (ITERS, len(RELAYED), layer_count, side // 2, side),
     ]
+    relays = pltpu.SemaphoreType.DMA((ITERS, len(RELAYED), layer_count))
     sems = (ITERS, len(PHASES), layer_count, 2)
     return pl.pallas_call(
         functools.partial(step_kernel, shape),
@@ -323,13 +387,16 @@
         scratch_shapes=[pltpu.VMEM(tables.shape, jnp.bfloat16)]
         + [pltpu.VMEM(size, jnp.float32) for size in shapes]
         + [
+            relays,
+            relays,
+            relays,
             pltpu.SemaphoreType.DMA(sems),
             pltpu.SemaphoreType.DMA(sems),
             pltpu.SemaphoreType.DMA,
         ],
         compiler_params=pltpu.CompilerParams(collective_id=0, has_side_effects=True),
         name="steps",
-    )(object_field, probe, samples, corners, count, jnp.asarray(tables))
+    )(object_field, probe, samples, positions, counts, jnp.asarray(tables))
 
 
 def solution(mesh):

time: 65.9 us -> 65 us (0.986)
  the two profiles are of different devices: /device:TPU:15 before, /device:TPU:18 now
where the time goes in v3:
time: 65 us; the launch traced here: 64.8 us
  Pallas kernels  62.4 us (96%)
  local copies, waits for them, and re-layouts  1.77 us (3%)
  between operations  0.66 us (1%)
    pallas_call x1, Pallas kernels, shards(): pl.pallas_call(functools.partial(step_kernel, shape), out_shape=jax.Shape...  62.4 us
    unnamed x1, local copies, waits for them, and re-layouts  1.77 us

profile of v3, /device:TPU:18, one launch (start us, length us, event | category | flops | bytes accessed | tf_op | source)
XLA Modules:
  0.0 64.8 jit_solution(8809285570235446433)
XLA Ops:
  0.7 62.4 %steps.1 = f32[3,2,128,128]{3,2,1,0:T(8,128)} custom-call(f32[3,2,128,128]{3,2,1,0:T(8,128)} %field.1, f32[2,128,128]{2,1,0:T(8,128)} %probe.1, f32[2,128,128]{2,1,0:T(8,128)} %bitcast.1, s32[1,1,2,2]{3,2,1,0:T(2,128)} %corners.1, s32[1,1]{1,0:T(1,128)S(6)} %copy.8.count, bf16[4,2,256,256]{3,2,1,0:T(8,128)(2,1)} %constant.2.clone.table_far), custom_call_target="tpu_custom_call" | custom-call | tf_op jit(solution)/shard_map/steps/pallas_call | solution.py:382
  63.1 1.8 %copy.9 = f32[3,2,128,128]{3,2,1,0:T(8,128)} copy(f32[3,2,128,128]{3,2,1,0:T(8,128)} %steps.1) | data formatting | bytes 786432
